TPU v7x, 256 devices: a whole 4x4x8 slice. The times are simulated.
256 devices in a mesh: samp: 32 (over z, y_hi, core), snp: 8 (over y_lo, x).
Axes of the slice: x: 4, y: 4 (y_hi: 2, y_lo: 2; y = y_hi * 2 + y_lo), z: 8, core: 2. Of those that a mesh axis runs over, the one named last changes fastest.
Arguments:
- genotypes: float32 [8192, 8192], P('samp', 'snp'), may hold values from 0 to 2, as said below
- observed: int32 [8192, 8192], P('samp', 'snp'), may hold values from 0 to 1
Outputs:
- relation: float32 [32, 8, 32, 8192], P(None, 'snp', None, 'samp')
Inputs may be any that keep to these rules, and one draw needn't show every extreme that they name: `genotypes`: dosages are real numbers between 0 and 2.
All inputs are finite; a program needn't handle non-finite values.
Results may differ from a plain program's by a relative error of at most 0.00061.
Values may be sent and summed in bfloat16 or wider, within the bound.
No kernel may reach another device: no remote copies, remote signals or barrier semaphores. Data moves between devices by JAX's collectives and lax.ppermute only.
A program may use at most 128 MiB of HBM per device.

v0:
```python
import jax
import jax.numpy as jnp
from jax import lax
from jax.sharding import PartitionSpec as P

var_floor = 0.1


def from_everyone(x, axis):
    devices = lax.axis_size(axis)
    return lax.all_to_all(jnp.broadcast_to(x[None], (devices, *x.shape)), axis, 0, 0, tiled=True)


def taken_together(x, axis):
    everything = from_everyone(x, axis)
    return jnp.sum(everything, axis=0)


def together(arrays, axis):
    ends = [0]
    for a in arrays:
        ends.append(ends[-1] + a.size)
    total = taken_together(jnp.concatenate([a.ravel() for a in arrays]), axis)
    return tuple((total[b:e].reshape(a.shape) for a, b, e in zip(arrays, ends, ends[1:])))


def body(genotypes, observed):
    row_count, snp_count = genotypes.shape
    present = observed.astype(jnp.float32)
    alt_local = jnp.sum(present * genotypes, axis=0)
    call_local = jnp.sum(present, axis=0)
    alt_sum, call_sum = together((alt_local, call_local), "samp")
    frequency = alt_sum / (2.0 * jnp.maximum(call_sum, 1.0))
    variance = jnp.maximum(2.0 * frequency * (1.0 - frequency), var_floor)
    scaled = (present * (genotypes - 2.0 * frequency) * lax.rsqrt(variance)).astype(jnp.bfloat16)
    shards = lax.axis_size("samp")
    groups = lax.axis_size("snp")
    tile_rows = row_count // groups
    total_snps = snp_count * groups
    own_panel = lax.all_gather(scaled, "snp", axis=1, tiled=True)
    blocks = scaled.reshape(groups, tile_rows, snp_count)
    owned_rows = lax.all_to_all(blocks, "snp", split_axis=0, concat_axis=2, tiled=True)
    owned_rows = owned_rows.reshape(tile_rows, total_snps)
    summed = lax.dot_general(
        lax.all_gather(owned_rows, "samp", axis=0, tiled=True),
        own_panel,
        (((1,), (1,)), ((), ())),
        preferred_element_type=jnp.float32,
    )
    summed = summed.reshape(shards, 1, tile_rows, row_count)
    return summed / total_snps


def solution(mesh):
    return jax.shard_map(
        body,
        mesh=mesh,
        in_specs=(P("samp", "snp"), P("samp", "snp")),
        out_specs=P(None, "snp", None, "samp"),
        check_vma=False,
    )
```

profile of v0, /device:TPU:1, one launch (start us, length us, event | category | flops | bytes accessed | tf_op | source)
XLA Modules:
  0.0 245.6 jit_solution(18037408167674693054)
XLA Ops:
  6.5 0.0 all-gather.5.cloned.1.call-start
  6.5 1.8 multiply_reduce_fusion
  8.3 0.1 broadcast_in_dim.2
  8.5 25.5 %all_to_all.21 = f32[32,1,2048]{2,1,0:T(1,128)S(1)} all-to-all(f32[32,1,2048]{2,1,0:T(1,128)S(1)} %broadcast_in_dim.2), channel_id=1, replica_groups=mesh['samp'=32,'snp'=8] {'samp'}, dimensions={0} | all-to-all | bytes 524288 | tf_op jit(solution)/shard_map/all_to_all | solution.py:11
  33.9 0.2 reduce_sum.29
  34.1 2.6 %multiply_convert_fusion = bf16[256,1024]{1,0:T(8,128)(2,1)} fusion(f32[256,1024]{1,0:T(8,128)} %param.2, s32[256,1024]{1,0:T(8,128)} %param.3, f32[1024]{0:T(1024)S(1)} %get-tuple-element.8, f32[1024]{0:T(1024)S(1)} %get-tuple-element.7), kind=kLoop, calls=%fused_computation.1 | loop fusion | flops 1310720 | bytes 2629632 | tf_op jit(solution)/shard_map/convert_element_type | solution.py:35
  36.7 0.0 all-gather.5.cloned.1.call-update
  36.7 0.0 all-gather.3.cloned.1.call-start
  36.8 15.4 %all_to_all.22 = bf16[8,32,1024]{2,1,0:T(8,128)(2,1)S(1)} all-to-all(bf16[8,32,1024]{2,1,0:T(8,128)(2,1)} %bitcast.14), channel_id=1, replica_groups=mesh['samp'=32,'snp'=8] {'snp'}, dimensions={0} | all-to-all | bytes 1048576 | tf_op jit(solution)/shard_map/all_to_all | solution.py:42
  52.1 0.8 copy.16
  53.0 0.0 all-gather.3.cloned.1.call-update
  53.0 38.4 %all-gather.5.cloned.1.call-done = bf16[256,8192]{1,0:T(8,128)(2,1)} async-done(((bf16[256,1024]{1,0:T(8,128)(2,1)}), bf16[256,8192]{1,0:T(8,128)(2,1)}) %all-gather.5.cloned.1.call-update) | async-done | bytes 4194320 | tf_op jit(solution)/shard_map/all_gather | solution.py:40
  91.4 135.0 %all-gather.3.cloned.1.call-done = bf16[1024,8192]{1,0:T(8,128)(2,1)} async-done(((bf16[32,8192]{1,0:T(8,128)(2,1)}), bf16[1024,8192]{1,0:T(8,128)(2,1)}) %all-gather.3.cloned.1.call-update) | async-done | bytes 16777232 | tf_op jit(solution)/shard_map/all_gather | solution.py:45
  226.3 12.5 %convolution_multiply_fusion = f32[1024,256]{1,0:T(8,128)} fusion(bf16[1024,8192]{1,0:T(8,128)(2,1)} %all-gather.3.cloned.1.call-done, bf16[256,8192]{1,0:T(8,128)(2,1)} %all-gather.5.cloned.1.call-done), kind=kOutput, calls=%fused_computation | convolution fusion | flops 4295229440 | bytes 22020096 | tf_op jit(solution)/shard_map/dot_general | solution.py:44
  (2 shorter events, 0.0 us)
Async XLA Ops:
  6.5 84.8 %all-gather.5.cloned.1.call-start = ((), (), s32[]{:S(2)}) async-start(), calls=%async_computation.3 | async-start | bytes 4718592 | tf_op jit(solution)/shard_map/all_gather | solution.py:40
  36.7 189.6 %all-gather.3.cloned.1.call-start = ((), (), s32[]{:S(2)}) async-start(), calls=%async_computation.2 | async-start | bytes 17301504 | tf_op jit(solution)/shard_map/all_gather | solution.py:45
Sparse Core Ops, SparseCore 0:
  36.8 54.4 all-gather.4
  94.1 132.1 all-gather.2
where the time goes:
time: 246 us
  waiting for transfers between devices  173 us (70%)
  blocking collectives  40.8 us (17%)
  between operations  13.4 us (5%)
  matrix products  12.5 us (5%)
  other arithmetic  4.52 us (2%)
    all_gather x1, waiting for transfers between devices, body(): lax.all_gather(owned_rows, 'samp', axis=0, tiled=True)  135 us
    all_gather x1, waiting for transfers between devices, body(): own_panel = lax.all_gather(scaled, 'snp', axis=1, tiled=True)  38.4 us
    all_to_all x1, blocking collectives, from_everyone(): lax.all_to_all(jnp.broadcast_to(x[None], (devices, *x.shape)), axis, 0, 0...  25.5 us
    all_to_all x1, blocking collectives, body(): lax.all_to_all(blocks, 'snp', split_axis=0, concat_axis=2, tiled=True)  15.4 us
    dot_general x1, matrix products, body(): lax.dot_general(lax.all_gather(owned_rows, 'samp', axis=0, tiled=True), o...  12.5 us
  transfers between devices with their start and end apart: 2, of which 2 were waited for; matrix products, arithmetic and copies ran while one was open for 0% of the time, Pallas kernels for 0%

commit v1 on v0

--- a/solution.py
+++ b/solution.py
@@ -37,7 +37,8 @@
     groups = lax.axis_size("snp")
     tile_rows = row_count // groups
     total_snps = snp_count * groups
-    own_panel = lax.all_gather(scaled, "snp", axis=1, tiled=True)
+    repeated = jnp.stack([scaled] * lax.axis_size("snp"))
+    own_panel = jnp.concatenate(lax.all_to_all(repeated, "snp", 0, 0), axis=1)
     blocks = scaled.reshape(groups, tile_rows, snp_count)
     owned_rows = lax.all_to_all(blocks, "snp", split_axis=0, concat_axis=2, tiled=True)
     owned_rows = owned_rows.reshape(tile_rows, total_snps)

time: 246 us -> 237 us (0.963)
  waiting for transfers between devices: 173 us -> 100 us
  blocking collectives: 40.8 us -> 93.1 us
  local copies, waits for them, and re-layouts: 0.97 us -> 13.2 us
    all_to_all x0 -> x1, blocking collectives: none -> 54.2 us  [body(): own_panel = jnp.concatenate(lax.all_to_all(repeated, 'snp', 0, 0), axis=1)]
    all_gather x1 -> x0, waiting for transfers between devices: 38.4 us -> none  [body(): own_panel = lax.all_gather(scaled, 'snp', axis=1, tiled=True)]
    all_gather x1, waiting for transfers between devices: 135 us -> 100 us  [body(): lax.all_gather(owned_rows, 'samp', axis=0, tiled=True)]
    reshape x0 -> x2, local copies, waits for them, and re-layouts: none -> 11.7 us  [body(): own_panel = jnp.concatenate(lax.all_to_all(repeated, 'snp', 0, 0), axis=1)]
  transfers between devices with their start and end apart: 2 -> 1, of which waited for: 2 -> 1; matrix products, arithmetic and copies ran while one was open for 0% -> 5% of each run, Pallas kernels for 0% -> 0%
where the time goes in v1:
time: 237 us; the launch traced here: 236 us
  waiting for transfers between devices  100 us (42%)
  blocking collectives  93.1 us (39%)
  between operations  13.4 us (6%)
  local copies, waits for them, and re-layouts  13.2 us (6%)
  matrix products  12.5 us (5%)
  other arithmetic  3.72 us (2%)
    all_gather x1, waiting for transfers between devices, body(): lax.all_gather(owned_rows, 'samp', axis=0, tiled=True)  100 us
    all_to_all x1, blocking collectives, body(): own_panel = jnp.concatenate(lax.all_to_all(repeated, 'snp', 0, 0), axis=1)  54.2 us
    all_to_all x1, blocking collectives, from_everyone(): lax.all_to_all(jnp.broadcast_to(x[None], (devices, *x.shape)), axis, 0, 0...  25.5 us
    all_to_all x1, blocking collectives, body(): lax.all_to_all(blocks, 'snp', split_axis=0, concat_axis=2, tiled=True)  13.4 us
    dot_general x1, matrix products, body(): lax.dot_general(lax.all_gather(owned_rows, 'samp', axis=0, tiled=True), o...  12.5 us
    reshape x2, local copies, waits for them, and re-layouts, body(): own_panel = jnp.concatenate(lax.all_to_all(repeated, 'snp', 0, 0), axis=1)  11.7 us
  transfers between devices with their start and end apart: 1, of which 1 were waited for; matrix products, arithmetic and copies ran while one was open for 5% of the time, Pallas kernels for 0%

profile of v1, /device:TPU:1, one launch (start us, length us, event | category | flops | bytes accessed | tf_op | source)
XLA Modules:
  0.0 236.1 jit_solution(14681781119131452409)
XLA Ops:
  6.5 0.0 all-gather.2.cloned.1.call-start
  6.5 1.8 multiply_reduce_fusion
  8.3 0.1 broadcast_in_dim.2
  8.5 25.5 %all_to_all.26 = f32[32,1,2048]{2,1,0:T(1,128)S(1)} all-to-all(f32[32,1,2048]{2,1,0:T(1,128)S(1)} %broadcast_in_dim.2), channel_id=1, replica_groups=mesh['samp'=32,'snp'=8] {'samp'}, dimensions={0} | all-to-all | bytes 524288 | tf_op jit(solution)/shard_map/all_to_all | solution.py:11
  33.9 0.2 reduce_sum.29
  34.1 1.8 multiply_convert_fusion
  35.9 13.4 %all_to_all.27 = bf16[8,32,1024]{2,1,0:T(8,128)(2,1)S(1)} all-to-all(bf16[8,32,1024]{2,1,0:T(8,128)(2,1)S(1)} %bitcast.18), channel_id=1, replica_groups=mesh['samp'=32,'snp'=8] {'snp'}, dimensions={0} | all-to-all | bytes 1048576 | tf_op jit(solution)/shard_map/all_to_all | solution.py:43
  49.3 0.8 copy.18
  50.1 0.0 all-gather.2.cloned.1.call-update
  50.1 0.5 stack.2
  50.7 54.2 %all_to_all.28 = bf16[8,256,1024]{2,1,0:T(8,128)(2,1)S(1)} all-to-all(bf16[8,256,1024]{2,1,0:T(8,128)(2,1)S(1)} %stack.2), channel_id=1, replica_groups=mesh['samp'=32,'snp'=8] {'snp'}, dimensions={0} | all-to-all | bytes 8388608 | tf_op jit(solution)/shard_map/all_to_all | solution.py:41
  104.9 4.3 %copy.13 = bf16[256,8,1024]{2,1,0:T(8,128)(2,1)} copy(bf16[256,8,1024]{2,0,1:T(8,128)(2,1)S(1)} %bitcast.17) | data formatting | bytes 8388608 | tf_op jit(solution)/shard_map/reshape | solution.py:41
  109.2 7.4 %reshape.31 = bf16[256,8192,1]{1,0,2:T(8,128)(2,1)} reshape(bf16[256,8,1024]{2,1,0:T(8,128)(2,1)} %copy.13) | data formatting | bytes 8388608 | tf_op jit(solution)/shard_map/reshape | solution.py:41
  116.6 100.2 %all-gather.2.cloned.1.call-done = bf16[1024,8192]{1,0:T(8,128)(2,1)} async-done(((bf16[32,8192]{1,0:T(8,128)(2,1)}), bf16[1024,8192]{1,0:T(8,128)(2,1)}) %all-gather.2.cloned.1.call-update) | async-done | bytes 16777232 | tf_op jit(solution)/shard_map/all_gather | solution.py:46
  216.8 12.5 %fusion = f32[32,1,32,256]{3,2,1,0:T(8,128)} fusion(bf16[32,32,8192]{2,1,0:T(8,128)(2,1)} %bitcast.21, bf16[256,8192,1]{1,0,2:T(8,128)(2,1)} %reshape.31), kind=kOutput, calls=%fused_computation.1 | convolution fusion | flops 4295229440 | bytes 22020096 | tf_op jit(solution)/shard_map/dot_general | solution.py:45
  (2 shorter events, 0.0 us)
Async XLA Ops:
  6.5 210.3 %all-gather.2.cloned.1.call-start = ((), (), s32[]{:S(2)}) async-start(), calls=%async_computation.3 | async-start | bytes 17301504 | tf_op jit(solution)/shard_map/all_gather | solution.py:46
Sparse Core Ops, SparseCore 0:
  50.3 166.4 all-gather.1
